TPU v7x, 32 devices: a whole 2x2x4 slice. The times are simulated.
32 devices in a mesh: rows: 8 (over z, x), grid: 4 (over y, core).
Axes of the slice: x: 2, y: 2, z: 4, core: 2. Of those that a mesh axis runs over, the one named last changes fastest.
Arguments:
- design: bfloat16 [98304, 1024], P(('rows', 'grid')), may hold values from -6 to 6
- observed: float32 [98304], P(('rows', 'grid')), may hold values from -6 to 6
- weight_class: int32 [98304], P(('rows', 'grid')), may hold values from 0 to 15
- calib_unit: int32 [98304], P(('rows', 'grid')), may hold values from 0 to 63
- class_weight: float32 [16], replicated, may hold values from 0.5 to 8
- calib_scale: float32 [64, 8], replicated, may hold values from 0.5 to 2
Outputs:
- normal_matrix: float32 [1024, 1024], P('rows', 'grid')
- right_hand: float32 [1024], P(('rows', 'grid'))
- chi_square: float32 [], replicated
All inputs are finite; a program needn't handle non-finite values.
Results may differ from a plain program's by a relative error of at most 0.01.
Values sent between devices are 32-bit elements; how exact they have to be, the bound alone decides.
A program may use at most 64 MiB of HBM per device.

v0:
```python
import jax
import jax.numpy as jnp
from jax import lax
from jax.sharding import PartitionSpec as P


def local(design, observed, weight_class, calib_unit, class_weight, calib_scale):
    row_count = design.shape[0]
    width = design.shape[1]
    blocks = calib_scale.shape[1]
    block_width = width // blocks
    count_rows = lax.axis_size("rows")
    count_grid = lax.axis_size("grid")
    total_rows = row_count * count_rows * count_grid
    class_hot = (
        weight_class[:, None] == jnp.arange(class_weight.shape[0], dtype=jnp.int32)[None, :]
    ).astype(jnp.float32)
    row_weight = jnp.dot(class_hot, class_weight, precision=lax.Precision.HIGHEST)
    root_weight = jnp.sqrt(row_weight)
    unit_hot = (
        calib_unit[:, None] == jnp.arange(calib_scale.shape[0], dtype=jnp.int32)[None, :]
    ).astype(jnp.float32)
    row_scales = jnp.dot(unit_hot, calib_scale, precision=lax.Precision.HIGHEST)
    scaled = (
        (
            design.reshape(row_count, blocks, block_width).astype(jnp.float32)
            * row_scales[:, :, None]
        )
        .reshape(row_count, width)
        .astype(jnp.bfloat16)
    )
    weighted = (root_weight[:, None] * scaled.astype(jnp.float32)).astype(jnp.bfloat16)
    term = lax.dot_general(
        weighted, weighted, (((0,), (0,)), ((), ())), preferred_element_type=jnp.float32
    )
    columns = lax.psum_scatter(term, "grid", scatter_dimension=1, tiled=True)
    gram = lax.psum_scatter(columns, "rows", scatter_dimension=0, tiled=True)
    weighted_obs = (root_weight * observed).astype(jnp.bfloat16)
    rhs_term = jnp.dot(weighted_obs, weighted, preferred_element_type=jnp.float32)
    chi_term = jnp.sum(row_weight * observed * observed)
    right_hand = lax.psum_scatter(rhs_term, ("rows", "grid"), scatter_dimension=0, tiled=True)
    chi_total = lax.psum(chi_term, ("rows", "grid"))
    return (gram / total_rows, right_hand / total_rows, chi_total / total_rows)


def solution(mesh):
    return jax.shard_map(
        local,
        mesh=mesh,
        in_specs=(
            P(("rows", "grid"), None),
            P(("rows", "grid")),
            P(("rows", "grid")),
            P(("rows", "grid")),
            P(),
            P(),
        ),
        out_specs=(P("rows", "grid"), P(("rows", "grid")), P()),
        check_vma=False,
    )
```

profile of v0, /device:TPU:4, one launch (start us, length us, event | category | flops | bytes accessed | tf_op | source)
XLA Modules:
  0.0 152.3 jit_solution(13866846923034456382)
XLA Ops:
  7.2 0.0 copy-start
  7.2 0.0 reduce-scatter.3.cloned.1.call-start
  7.2 0.9 fusion.3
  8.1 1.3 fusion.5
  9.4 0.0 copy-done
  9.4 0.0 slice-start
  9.4 3.2 %fusion.1 = f32[3072,8]{1,0:T(8,128)S(1)} fusion(f32[64,8]{0,1:T(8,128)S(1)} %copy-done, s32[3072]{0:T(1024)} %param.9), kind=kOutput, calls=%fused_computation.4 | convolution fusion | flops 19070976 | bytes 112640 | tf_op jit(solution)/shard_map/dot_general | solution.py:23
  12.7 0.0 slice-start.1
  12.7 3.5 %mul.29 = f32[3072,8,128]{2,1,0:T(8,128)S(1)} broadcast(f32[3072,8]{1,0:T(8,128)S(1)} %fusion.1), dimensions={0,1} | broadcast | bytes 12681216 | tf_op jit(solution)/shard_map/mul | solution.py:26
  16.2 0.0 slice-done
  16.2 0.0 slice-done.1
  16.2 2.2 %multiply_convert_fusion = bf16[3072,1024]{1,0:T(8,128)(2,1)S(1)} fusion(f32[384,8,8,128]{3,2,1,0:T(8,128)S(1)} %bitcast.17, bf16[3072,1024]{1,0:T(8,128)(2,1)S(1)} %bitcast.19, f32[3072]{0:T(1024)S(1)} %get-tuple-element.7), kind=kLoop, calls=%fused_computation.2 | loop fusion | flops 18874368 | bytes 25178112 | tf_op jit(solution)/shard_map/convert_element_type | solution.py:32
  18.4 0.0 copy-start.1
  18.4 2.6 %copy-done.1 = bf16[3072,1024]{1,0:T(8,128)(2,1)} copy-done((bf16[3072,1024]{1,0:T(8,128)(2,1)}, bf16[3072,1024]{1,0:T(8,128)(2,1)S(1)}, u32[]{:S(2)}) %copy-start.1) | copy-done | bytes 6291480
  21.0 8.3 %fusion.7 = f32[1024,1024]{1,0:T(8,128)} fusion(bf16[3072,1024]{1,0:T(8,128)(2,1)S(1)} %multiply_convert_fusion), kind=kOutput, calls=%fused_computation.15 | convolution fusion | flops 6442450944 | bytes 10485760 | tf_op jit(solution)/shard_map/dot_general | solution.py:33
  29.3 0.0 reduce-scatter.3.cloned.1.call-update
  29.3 0.0 reduce-scatter.5.cloned.1.call-start
  29.4 44.6 %reduce-scatter.3.cloned.1.call-done = f32[1024,256]{1,0:T(8,128)} async-done(((f32[1024,1024]{1,0:T(8,128)}), f32[1024,256]{1,0:T(8,128)}) %reduce-scatter.3.cloned.1.call-update) | async-done | bytes 1048592 | tf_op jit(solution)/shard_map/reduce_scatter | solution.py:36
  74.0 0.0 reduce-scatter.5.cloned.1.call-update
  74.0 3.7 %fusion.8 = f32[1,1024]{1,0:T(1,128)S(1)} fusion(bf16[3072,1]{0,1:T(2,128)(2,1)S(1)} %reshape.15, bf16[3072,1024]{1,0:T(8,128)(2,1)} %copy-done.1), kind=kOutput, calls=%fused_computation.16 | convolution fusion | flops 6291456 | bytes 6301696 | tf_op jit(solution)/shard_map/dot_general | solution.py:39
  77.8 41.8 %all-reduce.1 = (f32[1024]{0:T(1024)S(1)}, f32[]{:T(128)}) all-reduce(f32[1024]{0:T(1024)S(1)} %bitcast.20, f32[]{:T(128)} %get-tuple-element.5), channel_id=4, replica_groups=mesh['rows'=8,'grid'=4] {'rows','grid'}, use_global_device_ids=true, to_apply=%region_2.0.clone | all-reduce | flops 1025 | bytes 8200
  120.2 0.6 dynamic-slice_multiply_fusion
  120.8 21.9 %reduce-scatter.5.cloned.1.call-done = f32[128,256]{1,0:T(8,128)} async-done(((f32[1024,256]{1,0:T(8,128)}), f32[128,256]{1,0:T(8,128)}) %reduce-scatter.5.cloned.1.call-update) | async-done | bytes 131088 | tf_op jit(solution)/shard_map/reduce_scatter | solution.py:37
  142.8 1.6 %broadcast_multiply_fusion = f32[128,256]{1,0:T(8,128)} fusion(f32[128,256]{1,0:T(8,128)} %reduce-scatter.5.cloned.1.call-done), kind=kLoop, calls=%fused_computation.9 | loop fusion | flops 32768 | bytes 262144 | tf_op jit(solution)/shard_map/div | solution.py:43
  (2 shorter events, 0.0 us)
Async XLA Ops:
  7.2 2.3 %copy-start = (f32[64,8]{0,1:T(8,128)S(1)}, f32[64,8]{0,1:T(8,128)}, u32[]{:S(2)}) copy-start(f32[64,8]{0,1:T(8,128)} %param.11) | copy-start | bytes 6148
  7.2 66.8 %reduce-scatter.3.cloned.1.call-start = ((), (), s32[]{:S(2)}) async-start(), calls=%async_computation.2 | async-start | bytes 5242880 | tf_op jit(solution)/shard_map/reduce_scatter | solution.py:36
  9.4 6.7 %slice-start = ((s8[6291456]{0:T(1024)(128)(4,1)}), s8[4194304]{0:T(1024)(128)(4,1)S(1)}, s32[]{:S(2)}) async-start(s8[6291456]{0:T(1024)(128)(4,1)} %bitcast.18), calls=%async_computation.4 | async-start | bytes 8388608
  12.7 3.5 %slice-start.1 = ((s8[6291456]{0:T(1024)(128)(4,1)}), s8[2097152]{0:T(1024)(128)(4,1)S(1)}, s32[]{:S(2)}) async-start(s8[6291456]{0:T(1024)(128)(4,1)} %bitcast.18), calls=%async_computation.5 | async-start | bytes 4194304
  18.4 2.6 %copy-start.1 = (bf16[3072,1024]{1,0:T(8,128)(2,1)}, bf16[3072,1024]{1,0:T(8,128)(2,1)S(1)}, u32[]{:S(2)}) copy-start(bf16[3072,1024]{1,0:T(8,128)(2,1)S(1)} %multiply_convert_fusion) | copy-start | bytes 18874372
  29.3 113.4 %reduce-scatter.5.cloned.1.call-start = ((), (), s32[]{:S(2)}) async-start(), calls=%async_computation.3 | async-start | bytes 1179648 | tf_op jit(solution)/shard_map/reduce_scatter | solution.py:37
Sparse Core Ops, SparseCore 0:
  29.5 44.4 reduce-scatter.2
  77.4 65.3 reduce-scatter.4
where the time goes:
time: 154 us; the launch traced here: 152 us
  waiting for transfers between devices  66.6 us (43%)
  blocking collectives  41.8 us (27%)
  matrix products  16.1 us (10%)
  between operations  15.9 us (10%)
  local copies, waits for them, and re-layouts  6.12 us (4%)
  other arithmetic  5.65 us (4%)
    reduce_scatter x1, waiting for transfers between devices, local(): columns = lax.psum_scatter(term, 'grid', scatter_dimension=1, tiled=True)  44.6 us
    unnamed x1, blocking collectives  41.8 us
    reduce_scatter x1, waiting for transfers between devices, local(): gram = lax.psum_scatter(columns, 'rows', scatter_dimension=0, tiled=True)  21.9 us
    dot_general x1, matrix products, local(): lax.dot_general(weighted, weighted, (((0,), (0,)), ((), ())), preferred_e...  8.31 us
    dot_general x1, matrix products, local(): jnp.dot(weighted_obs, weighted, preferred_element_type=jnp.float32)  3.71 us
    mul x1, local copies, waits for them, and re-layouts, local(): design.reshape(row_count, blocks, block_width).astype(jnp.float32)  3.46 us
    dot_general x1, matrix products, local(): row_scales = jnp.dot(unit_hot, calib_scale, precision=lax.Precision.HIGHEST)  3.23 us
  transfers between devices with their start and end apart: 2, of which 2 were waited for; matrix products, arithmetic and copies ran while one was open for 3% of the time, Pallas kernels for 0%

commit v1 on v0

v1 whole, which is shorter than its diff:
```python
import functools

import jax
import jax.numpy as jnp
from jax import lax
from jax.experimental import pallas as pl
from jax.experimental.pallas import tpu as pltpu
from jax.sharding import PartitionSpec as P

MESH = pl.DeviceIdType.MESH
LANES = 128
F32 = jnp.float32
BF16 = jnp.bfloat16


def plain(design, observed, weight_class, calib_unit, class_weight, calib_scale):
    row_count, width = design.shape
    blocks = calib_scale.shape[1]
    total_rows = row_count * lax.axis_size("rows") * lax.axis_size("grid")
    class_hot = (
        weight_class[:, None] == jnp.arange(class_weight.shape[0], dtype=jnp.int32)[None, :]
    ).astype(F32)
    row_weight = jnp.dot(class_hot, class_weight, precision=lax.Precision.HIGHEST)
    root_weight = jnp.sqrt(row_weight)
    unit_hot = (
        calib_unit[:, None] == jnp.arange(calib_scale.shape[0], dtype=jnp.int32)[None, :]
    ).astype(F32)
    row_scales = jnp.dot(unit_hot, calib_scale, precision=lax.Precision.HIGHEST)
    scaled = (
        (design.reshape(row_count, blocks, width // blocks).astype(F32) * row_scales[:, :, None])
        .reshape(row_count, width)
        .astype(BF16)
    )
    weighted = (root_weight[:, None] * scaled.astype(F32)).astype(BF16)
    term = lax.dot_general(weighted, weighted, (((0,), (0,)), ((), ())), preferred_element_type=F32)
    columns = lax.psum_scatter(term, "grid", scatter_dimension=1, tiled=True)
    gram = lax.psum_scatter(columns, "rows", scatter_dimension=0, tiled=True)
    weighted_obs = (root_weight * observed).astype(BF16)
    rhs_term = jnp.dot(weighted_obs, weighted, preferred_element_type=F32)
    chi_term = jnp.sum(row_weight * observed * observed)
    right_hand = lax.psum_scatter(rhs_term, ("rows", "grid"), scatter_dimension=0, tiled=True)
    chi_total = lax.psum(chi_term, ("rows", "grid"))
    return (gram / total_rows, right_hand / total_rows, chi_total / total_rows)


def split3(value):
    high = value.astype(BF16)
    rest = value - high.astype(F32)
    middle = rest.astype(BF16)
    low = (rest - middle.astype(F32)).astype(BF16)
    return high, middle, low


def kernel(
    dims,
    design_hbm, obs_ref, class_ref, unit_ref, cw_ref, cs_ref,
    gram_ref, aux_ref,
    raw, weighted, table, cwcol, rhs_acc, chi_acc,
    buf, rx0, s1, rx1, s2, rx2, s3, rx3, fin, ext, mrx, erx, axs, rxa,
    in_sem, q0, r0, q1, r1, q2, r2, q3, r3, qm, rm, qe, re, qa, ra,
):
    n_rows, n_grid, total_rows = dims
    n_z = n_rows // 2
    row_count, width = raw.shape
    units = cs_ref.shape[0]
    blocks = cs_ref.shape[1]
    classes = cw_ref.shape[0]
    half = LANES // 2
    piece = LANES // (2 * n_grid)
    sub = piece // 2
    r = lax.axis_index("rows")
    g = lax.axis_index("grid")
    z = r // 2
    x = lax.rem(r, 2)
    y = g // 2
    c = lax.rem(g, 2)
    me = r * n_grid + g
    count = n_rows * n_grid

    n_chunks = in_sem.shape[0]
    chunk = row_count // n_chunks
    loads = [
        pltpu.make_async_copy(
            design_hbm.at[pl.ds(k * chunk, chunk)], raw.at[pl.ds(k * chunk, chunk)], in_sem.at[k]
        )
        for k in range(n_chunks)
    ]
    for load in loads:
        load.start()

    barrier = pltpu.get_barrier_semaphore()

    def greet(k, carry):
        flat = lax.rem(me + k, count)
        pl.semaphore_signal(
            barrier, inc=1, device_id=(flat // n_grid, lax.rem(flat, n_grid)), device_id_type=MESH
        )
        return carry

    lax.fori_loop(1, count, greet, 0)

    depth = table.shape[0]
    table[...] = jnp.zeros_like(table)
    for b in range(blocks):
        wide = jnp.broadcast_to(cs_ref[:, b : b + 1], (units, LANES))
        for t, term in enumerate(split3(wide)):
            table[t * units : (t + 1) * units, b * LANES : (b + 1) * LANES] = term
    index = lax.broadcasted_iota(jnp.int32, (classes, LANES), 0)
    weights = jnp.zeros((classes, LANES), F32)
    for k in range(classes):
        weights = jnp.where(index == k, cw_ref[k], weights)
    cwcol[...] = weights
    for t, term in enumerate(split3(jnp.sqrt(weights))):
        at = 3 * units + t * classes
        table[at : at + classes, width : width + LANES] = term
    obs_at = 3 * (units + classes)
    tail = depth - obs_at
    obs_index = lax.broadcasted_iota(jnp.int32, (tail, LANES), 0)
    table[obs_at:, width + LANES :] = jnp.where(obs_index < 3, 1.0, 0.0).astype(BF16)
    rhs_acc[...] = jnp.zeros_like(rhs_acc)
    chi_acc[...] = jnp.zeros_like(chi_acc)
    unit_index = lax.broadcasted_iota(jnp.int32, (units, LANES), 0)

    def prepare(step):
        at = pl.multiple_of(step * LANES, LANES)
        unit_row = unit_ref[pl.ds(step, 1), :]
        class_row = class_ref[pl.ds(step, 1), :]
        obs_row = obs_ref[pl.ds(step, 1), :]
        unit_hot = jnp.where(unit_index == unit_row, 1.0, 0.0).astype(BF16)
        is_class = index == class_row
        class_hot = jnp.where(is_class, 1.0, 0.0).astype(BF16)
        row_weight = jnp.sum(jnp.where(is_class, cwcol[...], 0.0), axis=0, keepdims=True)
        chi_acc[0:1, :] += row_weight * obs_row * obs_row
        o0, o1, o2 = [t.astype(F32) for t in split3(obs_row)]
        obs_rows = jnp.where(
            obs_index == 0, o0, jnp.where(obs_index == 1, o1, jnp.where(obs_index == 2, o2, 0.0))
        ).astype(BF16)
        hot = jnp.concatenate([unit_hot] * 3 + [class_hot] * 3 + [obs_rows], axis=0)
        looked = lax.dot_general(
            hot, table[...], (((0,), (0,)), ((), ())), preferred_element_type=F32
        )
        root = looked[:, width : width + LANES]
        wobs = root * looked[:, width + LANES :]
        for b in range(width // LANES):
            cols = slice(b * LANES, (b + 1) * LANES)
            value = raw[pl.ds(at, LANES), cols].astype(F32) * (looked[:, cols] * root)
            rounded = value.astype(BF16)
            weighted[pl.ds(at, LANES), cols] = rounded
            part = (rounded.astype(F32) * wobs).reshape(LANES // 8, 8, LANES)
            rhs_acc[:, cols] += jnp.sum(part, axis=0)

    per_chunk = chunk // LANES
    for k in range(n_chunks):
        loads[k].wait()

        def body(i, carry):
            prepare(k * per_chunk + i)
            return carry

        lax.fori_loop(0, per_chunk, body, 0)

    def remote(src, dst, send, recv, device):
        return pltpu.make_async_remote_copy(
            src_ref=src, dst_ref=dst, send_sem=send, recv_sem=recv,
            device_id=device, device_id_type=MESH,
        )

    across_core = (r, y * 2 + 1 - c)
    across_x = (z * 2 + 1 - x, g)
    across_y = (r, (1 - y) * 2 + c)
    axis_of = ((across_x, x), (across_y, y))

    for b in range(width // LANES):
        axs[0, b : b + 1, :] = jnp.sum(rhs_acc[:, b * LANES : (b + 1) * LANES], axis=0, keepdims=True)
    axs[0, n_rows:, :] = jnp.broadcast_to(jnp.sum(chi_acc[0:1, :], axis=1, keepdims=True), (8, LANES))
    pl.semaphore_wait(barrier, count - 1)
    small = [remote(axs.at[0], rxa.at[0], qa.at[0], ra.at[0], across_core)]
    small[0].start()

    def small_step(k, device):
        small[k - 1].wait_recv()
        axs[k] = axs[k - 1] + rxa[k - 1]
        if device is not None:
            copy = remote(axs.at[k], rxa.at[k], qa.at[k], ra.at[k], device)
            copy.start()
            small.append(copy)

    def other_z(k):
        return lax.rem(z + k, n_z)

    def gram_panel(a):
        lo = 2 * a * LANES
        for b in range(a, n_z):
            tile = lax.dot_general(
                weighted[:, lo : lo + 2 * LANES], weighted[:, 2 * b * LANES : 2 * (b + 1) * LANES],
                (((0,), (0,)), ((), ())), preferred_element_type=F32,
            )
            for u in range(2):
                for v in range(2):
                    i, j = 2 * a + u, 2 * b + v
                    if i > j:
                        continue
                    block = tile[u * LANES : (u + 1) * LANES, v * LANES : (v + 1) * LANES]
                    if j == i + 1 and a == b:
                        for q in range(2 * n_grid):
                            dr, dg = 2 * a + q // n_grid, q % n_grid
                            for p in range(2):
                                first, second = (dr % 2, dg // 2) if p == 0 else (dg // 2, dr % 2)
                                at = q * piece + p * sub
                                buf[dr // 2, p, dg % 2, first, second, half : half + sub, :] = block[at : at + sub]
                        continue
                    if i == j or (i + j) % 2 == 1:
                        dr, dg = i, j // 2
                    else:
                        dr, dg = j, i // 2
                    for p in range(2):
                        first, second = (dr % 2, dg // 2) if p == 0 else (dg // 2, dr % 2)
                        buf[dr // 2, p, dg % 2, first, second, 0:half, :] = block[p * half : (p + 1) * half]

    def copy0(a, p):
        return remote(buf.at[a, p, 1 - c], rx0.at[a, p], q0.at[a, p], r0.at[a, p], across_core)

    def copy1(a, p):
        return remote(s1.at[a, p], rx1.at[a, p], q1.at[a, p], r1.at[a, p], axis_of[p][0])

    def copy2(a, p):
        return remote(s2.at[a, p], rx2.at[a, p], q2.at[a, p], r2.at[a, p], axis_of[1 - p][0])

    def copy3(a):
        return remote(s3.at[a], rx3.at[z], q3.at[a], r3.at[z], (a * 2 + x, g))

    def stage0(a):
        for p in range(2):
            copy0(a, p).start()

    def stage1(a):
        for p in range(2):
            first = axis_of[p][1]
            copy0(a, p).wait_recv()
            s1[a, p] = buf[a, p, c, 1 - first] + rx0[a, p, 1 - first]
            copy1(a, p).start()

    def stage2(a):
        for p in range(2):
            first, second = axis_of[p][1], axis_of[1 - p][1]
            copy1(a, p).wait_recv()
            s2[a, p] = (
                buf[a, p, c, first, 1 - second] + rx0[a, p, first, 1 - second] + rx1[a, p, 1 - second]
            )
            copy2(a, p).start()

    def stage3(a):
        for p in range(2):
            first, second = axis_of[p][1], axis_of[1 - p][1]
            copy2(a, p).wait_recv()
            s3[a, p] = (
                buf[a, p, c, first, second] + rx0[a, p, first, second] + rx1[a, p, second] + rx2[a, p]
            )

        @pl.when(z != a)
        def _():
            copy3(a).start()

    gram_panel(0)
    stage0(0)
    small_step(1, across_x)
    gram_panel(1)
    stage0(1)
    stage1(0)
    gram_panel(2)
    stage0(2)
    stage1(1)
    gram_panel(3)
    stage0(3)
    stage1(3)
    small_step(2, across_y)
    stage2(0)
    stage1(2)
    stage2(1)
    stage3(0)
    small_step(3, None)
    spread = []
    for k in range(1, n_z):
        copy = remote(
            axs.at[3], rxa.at[3 + k], qa.at[3 + k], ra.at[3 + k], (other_z(k) * 2 + x, g)
        )
        copy.start()
        spread.append(copy)
    stage2(3)
    stage3(1)
    stage2(2)
    stage3(3)
    stage3(2)

    scale = 1.0 / total_rows
    for k in range(1, n_z):
        spread[k - 1].wait_recv()
    sums = axs[3]
    for k in range(1, n_z):
        sums = sums + rxa[3 + k]
    aux_ref[...] = sums * scale

    for k in range(1, n_z):
        from_z = other_z(k)
        remote(s3.at[from_z], rx3.at[from_z], q3.at[from_z], r3.at[from_z], (from_z * 2 + x, g)).wait_recv()
    for p in range(2):
        value = s3[z, p]
        for k in range(1, n_z):
            value = value + rx3[other_z(k), p]
        value = value * scale
        fin[p * half : (p + 1) * half, :] = value[0:half]
        ext[p * sub : (p + 1) * sub, :] = value[half : half + sub]

    a = z
    mine = x * n_grid + g
    diagonal = g == a
    owned = jnp.where(g > a, 1 - x, x)
    col_owned = pl.ds(pl.multiple_of(owned * LANES, LANES), LANES)
    col_other = pl.ds(pl.multiple_of((1 - owned) * LANES, LANES), LANES)
    mirror = remote(fin, mrx, qm, rm, (2 * g + owned, a))

    @pl.when(jnp.logical_not(diagonal))
    def _():
        mirror.start()

    def extra(k):
        return remote(ext, erx.at[mine], qe.at[k], re.at[mine], (2 * a + k, a))

    for k in range(2):
        @pl.when(jnp.logical_or(jnp.logical_not(diagonal), x != k))
        def _():
            extra(k).start()

    @pl.when(g > a)
    def _():
        gram_ref[:, col_owned] = fin[...]
        mirror.wait_recv()
        gram_ref[:, col_other] = mrx[...]

    @pl.when(g < a)
    def _():
        gram_ref[:, col_owned] = fin[...].T
        mirror.wait_recv()
        gram_ref[:, col_other] = mrx[...].T

    @pl.when(diagonal)
    def _():
        gram_ref[:, col_owned] = fin[...]
        erx[mine] = ext[...]
        for k in range(1, 2 * n_grid):
            q = lax.rem(mine + k, 2 * n_grid)
            remote(ext, erx.at[q], qe.at[0], re.at[q], (2 * a + 1 - x, a)).wait_recv()
        pair = erx[...].reshape(LANES, LANES)

        @pl.when(x == 0)
        def _():
            gram_ref[:, col_other] = pair

        @pl.when(x == 1)
        def _():
            gram_ref[:, col_other] = pair.T

    for copy in small + spread:
        copy.wait_send()
    for b in range(n_z):
        for p in range(2):
            copy0(b, p).wait_send()
            copy1(b, p).wait_send()
            copy2(b, p).wait_send()

        @pl.when(z != b)
        def _():
            copy3(b).wait_send()

    @pl.when(jnp.logical_not(diagonal))
    def _():
        mirror.wait_send()

    for k in range(2):
        @pl.when(jnp.logical_or(jnp.logical_not(diagonal), x != k))
        def _():
            extra(k).wait_send()


def fused(design, observed, weight_class, calib_unit, class_weight, calib_scale):
    n_rows = lax.axis_size("rows")
    n_grid = lax.axis_size("grid")
    row_count, width = design.shape
    n_z = n_rows // 2
    units, classes = calib_scale.shape[0], class_weight.shape[0]
    piece = LANES // (2 * n_grid)
    slot = LANES // 2 + piece // 2
    depth = 3 * (units + classes) + 16
    lines = row_count // LANES
    vmem = pl.BlockSpec(memory_space=pltpu.VMEM)
    dma = pltpu.SemaphoreType.DMA
    gram, aux = pl.pallas_call(
        functools.partial(kernel, (n_rows, n_grid, row_count * n_rows * n_grid)),
        out_shape=(
            jax.ShapeDtypeStruct((LANES, 2 * LANES), F32),
            jax.ShapeDtypeStruct((n_rows + 8, LANES), F32),
        ),
        in_specs=[
            pl.BlockSpec(memory_space=pl.ANY), vmem, vmem, vmem,
            pl.BlockSpec(memory_space=pltpu.SMEM), vmem,
        ],
        out_specs=(vmem, vmem),
        scratch_shapes=[
            pltpu.VMEM((row_count, width), BF16),
            pltpu.VMEM((row_count, width), BF16),
            pltpu.VMEM((depth, width + 2 * LANES), BF16),
            pltpu.VMEM((classes, LANES), F32),
            pltpu.VMEM((8, width), F32),
            pltpu.VMEM((8, LANES), F32),
            pltpu.VMEM((n_z, 2, 2, 2, 2, slot, LANES), F32),
            pltpu.VMEM((n_z, 2, 2, 2, slot, LANES), F32),
            pltpu.VMEM((n_z, 2, 2, slot, LANES), F32),
            pltpu.VMEM((n_z, 2, 2, slot, LANES), F32),
            pltpu.VMEM((n_z, 2, slot, LANES), F32),
            pltpu.VMEM((n_z, 2, slot, LANES), F32),
            pltpu.VMEM((n_z, 2, slot, LANES), F32),
            pltpu.VMEM((n_z, 2, slot, LANES), F32),
            pltpu.VMEM((LANES, LANES), F32),
            pltpu.VMEM((piece, LANES), F32),
            pltpu.VMEM((LANES, LANES), F32),
            pltpu.VMEM((2 * n_grid, piece, LANES), F32),
            pltpu.VMEM((4, n_rows + 8, LANES), F32),
            pltpu.VMEM((3 + n_z, n_rows + 8, LANES), F32),
            dma((6,)),
            dma((n_z, 2)), dma((n_z, 2)),
            dma((n_z, 2)), dma((n_z, 2)),
            dma((n_z, 2)), dma((n_z, 2)),
            dma((n_z,)), dma((n_z,)),
            dma(()), dma(()),
            dma((2,)), dma((2 * n_grid,)),
            dma((3 + n_z,)), dma((3 + n_z,)),
        ],
        compiler_params=pltpu.CompilerParams(
            collective_id=0, has_side_effects=True, vmem_limit_bytes=60 * 1024 * 1024
        ),
    )(
        design,
        observed.reshape(lines, LANES),
        weight_class.reshape(lines, LANES),
        calib_unit.reshape(lines, LANES),
        class_weight,
        calib_scale,
    )
    part = width // (n_rows * n_grid)
    flat = (lax.axis_index("rows") * n_grid + lax.axis_index("grid")) * part
    right_hand = lax.dynamic_slice(
        aux, (flat // LANES, lax.rem(flat, LANES)), (1, part)
    ).reshape(part)
    return gram, right_hand, aux[n_rows, 0]


def local(design, observed, weight_class, calib_unit, class_weight, calib_scale):
    n_rows = lax.axis_size("rows")
    n_grid = lax.axis_size("grid")
    row_count, width = design.shape
    units, blocks = calib_scale.shape
    classes = class_weight.shape[0]
    fits = (
        n_grid == 4
        and n_rows == 8
        and width == n_rows * LANES
        and width == blocks * LANES
        and row_count % (6 * LANES) == 0
        and units % 16 == 0
        and classes % 16 == 0
    )
    run = fused if fits else plain
    return run(design, observed, weight_class, calib_unit, class_weight, calib_scale)


def solution(mesh):
    return jax.shard_map(
        local,
        mesh=mesh,
        in_specs=(
            P(("rows", "grid"), None),
            P(("rows", "grid")),
            P(("rows", "grid")),
            P(("rows", "grid")),
            P(),
            P(),
        ),
        out_specs=(P("rows", "grid"), P(("rows", "grid")), P()),
        check_vma=False,
    )
```

time: 154 us -> 47.7 us (0.31)
  waiting for transfers between devices: 66.6 us -> 0 us
  blocking collectives: 41.8 us -> 0 us
  Pallas kernels: 0 us -> 41.3 us
  matrix products: 16.1 us -> 0 us
  between operations: 15.9 us -> 0.67 us
  other arithmetic: 5.65 us -> 0 us
    reduce_scatter x2 -> x0, waiting for transfers between devices: 66.5 us -> none  [the longest x1 44.6 us: local(): columns = lax.psum_scatter(term, 'grid', scatter_dimension=1, tiled=True)]
    unnamed x1 -> x0, blocking collectives: 41.8 us -> none
    pallas_call x0 -> x1, Pallas kernels: none -> 41.3 us  [fused(): pl.pallas_call(functools.partial(kernel, (n_rows, n_grid, row_count * n_r...]
    dot_general x4 -> x0, matrix products: 16.1 us -> none  [the longest x1 8.31 us: local(): lax.dot_general(weighted, weighted, (((0,), (0,)), ((), ())), preferred_e...]
    mul x1 -> x0, local copies, waits for them, and re-layouts: 3.46 us -> none  [local(): design.reshape(row_count, blocks, block_width).astype(jnp.float32)]
    convert_element_type x1 -> x0, other arithmetic: 2.17 us -> none  [local(): (root_weight[:, None] * scaled.astype(jnp.float32)).astype(jnp.bfloat16)]
    div x2 -> x0, other arithmetic: 2.16 us -> none  [local(): return (gram / total_rows, right_hand / total_rows, chi_total / total_rows)]
  transfers between devices with their start and end apart: 2 -> 0, of which waited for: 2 -> 0; matrix products, arithmetic and copies ran while one was open for 3% -> 0% of each run, Pallas kernels for 0% -> 0%
where the time goes in v1:
time: 47.7 us; the launch traced here: 47.4 us
  Pallas kernels  41.3 us (87%)
  local copies, waits for them, and re-layouts  5.41 us (11%)
  between operations  0.67 us (1%)
    pallas_call x1, Pallas kernels, fused(): pl.pallas_call(functools.partial(kernel, (n_rows, n_grid, row_count * n_r...  41.3 us
    unnamed x2, local copies, waits for them, and re-layouts  2.95 us
    reshape x1, local copies, waits for them, and re-layouts, fused(): right_hand = lax.dynamic_slice(aux, (flat // LANES, lax.rem(flat, LANES))...  1.27 us
    slice x1, local copies, waits for them, and re-layouts, fused(): return (gram, right_hand, aux[n_rows, 0])  1.19 us

profile of v1, /device:TPU:4, one launch (start us, length us, event | category | flops | bytes accessed | tf_op | source)
XLA Modules:
  0.0 47.4 jit_solution(13129350788113375955)
XLA Ops:
  0.7 1.4 %copy.9.cs_ref = f32[64,8]{1,0:T(8,128)} copy(f32[64,8]{0,1:T(8,128)} %param.11) | data formatting | bytes 4096 | tf_op args[5]
  2.0 41.3 %shard_map.85 = (f32[128,256]{1,0:T(8,128)}, f32[16,128]{1,0:T(8,128)}) custom-call(bf16[3072,1024]{1,0:T(8,128)(2,1)} %design_hbm.1, f32[24,128]{1,0:T(8,128)} %bitcast.6, s32[24,128]{1,0:T(8,128)} %bitcast.7, s32[24,128]{1,0:T(8,128)} %bitcast.8, f32[16]{0:T(128)} %cw_ref.1, f32[64,8]{1,0:T(8,128)} %copy.9.cs_ref), custom_call_target="tpu_custom_call" | custom-call | tf_op jit(solution)/shard_map/pallas_call | solution.py:397
  43.4 1.2 %slice.3 = f32[1,1]{1,0:T(1,128)} slice(f32[16,128]{1,0:T(8,128)} %get-tuple-element.6), slice={[8:9], [0:1]} | slice | bytes 8 | tf_op jit(solution)/shard_map/slice | solution.py:454
  44.6 1.3 %dynamic-slice_bitcast_fusion = f32[32]{0:T(128)} fusion(f32[16,128]{1,0:T(8,128)} %get-tuple-element.6, s32[]{:T(128)S(6)} %select_n.12, s32[]{:T(128)S(6)} %select_n.13), kind=kLoop, calls=%fused_computation | loop fusion | bytes 264 | tf_op jit(solution)/shard_map/reshape | solution.py:453
  45.8 1.6 %copy.11 = f32[128,256]{1,0:T(8,128)} copy(f32[128,256]{1,0:T(8,128)} %get-tuple-element.10) | data formatting | bytes 262144

commit v2 on v1

--- a/solution.py
+++ b/solution.py
@@ -9,6 +9,7 @@
 
 MESH = pl.DeviceIdType.MESH
 LANES = 128
+GROUP = 4
 F32 = jnp.float32
 BF16 = jnp.bfloat16
 
@@ -54,7 +55,7 @@
 def kernel(
     dims,
     design_hbm, obs_ref, class_ref, unit_ref, cw_ref, cs_ref,
-    gram_ref, aux_ref,
+    gram_ref,
     raw, weighted, table, cwcol, rhs_acc, chi_acc,
     buf, rx0, s1, rx1, s2, rx2, s3, rx3, fin, ext, mrx, erx, axs, rxa,
     in_sem, q0, r0, q1, r1, q2, r2, q3, r3, qm, rm, qe, re, qa, ra,
@@ -62,8 +63,7 @@
     n_rows, n_grid, total_rows = dims
     n_z = n_rows // 2
     row_count, width = raw.shape
-    units = cs_ref.shape[0]
-    blocks = cs_ref.shape[1]
+    blocks, units = cs_ref.shape
     classes = cw_ref.shape[0]
     half = LANES // 2
     piece = LANES // (2 * n_grid)
@@ -101,8 +101,13 @@
 
     depth = table.shape[0]
     table[...] = jnp.zeros_like(table)
+    eye = lax.broadcasted_iota(jnp.int32, (units, units), 0) == lax.broadcasted_iota(
+        jnp.int32, (units, units), 1
+    )
     for b in range(blocks):
-        wide = jnp.broadcast_to(cs_ref[:, b : b + 1], (units, LANES))
+        square = jnp.broadcast_to(cs_ref[b : b + 1, :], (units, units))
+        column = jnp.sum(jnp.where(eye, square, 0.0), axis=1, keepdims=True)
+        wide = jnp.broadcast_to(column, (units, LANES))
         for t, term in enumerate(split3(wide)):
             table[t * units : (t + 1) * units, b * LANES : (b + 1) * LANES] = term
     index = lax.broadcasted_iota(jnp.int32, (classes, LANES), 0)
@@ -122,20 +127,22 @@
     unit_index = lax.broadcasted_iota(jnp.int32, (units, LANES), 0)
 
     def prepare(step):
-        at = pl.multiple_of(step * LANES, LANES)
-        unit_row = unit_ref[pl.ds(step, 1), :]
-        class_row = class_ref[pl.ds(step, 1), :]
-        obs_row = obs_ref[pl.ds(step, 1), :]
-        unit_hot = jnp.where(unit_index == unit_row, 1.0, 0.0).astype(BF16)
-        is_class = index == class_row
-        class_hot = jnp.where(is_class, 1.0, 0.0).astype(BF16)
-        row_weight = jnp.sum(jnp.where(is_class, cwcol[...], 0.0), axis=0, keepdims=True)
-        chi_acc[0:1, :] += row_weight * obs_row * obs_row
-        o0, o1, o2 = [t.astype(F32) for t in split3(obs_row)]
-        obs_rows = jnp.where(
-            obs_index == 0, o0, jnp.where(obs_index == 1, o1, jnp.where(obs_index == 2, o2, 0.0))
-        ).astype(BF16)
-        hot = jnp.concatenate([unit_hot] * 3 + [class_hot] * 3 + [obs_rows], axis=0)
+        at = pl.multiple_of(step * (GROUP * LANES), GROUP * LANES)
+        hots = []
+        for u in range(GROUP):
+            line = pl.ds(step * GROUP + u, 1)
+            unit_row, class_row, obs_row = unit_ref[line, :], class_ref[line, :], obs_ref[line, :]
+            unit_hot = jnp.where(unit_index == unit_row, 1.0, 0.0).astype(BF16)
+            is_class = index == class_row
+            class_hot = jnp.where(is_class, 1.0, 0.0).astype(BF16)
+            row_weight = jnp.sum(jnp.where(is_class, cwcol[...], 0.0), axis=0, keepdims=True)
+            chi_acc[0:1, :] += row_weight * obs_row * obs_row
+            o0, o1, o2 = [t.astype(F32) for t in split3(obs_row)]
+            obs_rows = jnp.where(
+                obs_index == 0, o0, jnp.where(obs_index == 1, o1, jnp.where(obs_index == 2, o2, 0.0))
+            ).astype(BF16)
+            hots.append(jnp.concatenate([unit_hot] * 3 + [class_hot] * 3 + [obs_rows], axis=0))
+        hot = jnp.concatenate(hots, axis=1)
         looked = lax.dot_general(
             hot, table[...], (((0,), (0,)), ((), ())), preferred_element_type=F32
         )
@@ -143,13 +150,12 @@
         wobs = root * looked[:, width + LANES :]
         for b in range(width // LANES):
             cols = slice(b * LANES, (b + 1) * LANES)
-            value = raw[pl.ds(at, LANES), cols].astype(F32) * (looked[:, cols] * root)
-            rounded = value.astype(BF16)
-            weighted[pl.ds(at, LANES), cols] = rounded
-            part = (rounded.astype(F32) * wobs).reshape(LANES // 8, 8, LANES)
+            value = raw[pl.ds(at, GROUP * LANES), cols].astype(F32) * (looked[:, cols] * root)
+            weighted[pl.ds(at, GROUP * LANES), cols] = value.astype(BF16)
+            part = (value * wobs).reshape(GROUP * LANES // 8, 8, LANES)
             rhs_acc[:, cols] += jnp.sum(part, axis=0)
 
-    per_chunk = chunk // LANES
+    per_chunk = chunk // (GROUP * LANES)
     for k in range(n_chunks):
         loads[k].wait()
 
@@ -298,7 +304,7 @@
     sums = axs[3]
     for k in range(1, n_z):
         sums = sums + rxa[3 + k]
-    aux_ref[...] = sums * scale
+    gram_ref[LANES:, 0:LANES] = sums * scale
 
     for k in range(1, n_z):
         from_z = other_z(k)
@@ -333,19 +339,19 @@
 
     @pl.when(g > a)
     def _():
-        gram_ref[:, col_owned] = fin[...]
+        gram_ref[0:LANES, col_owned] = fin[...]
         mirror.wait_recv()
-        gram_ref[:, col_other] = mrx[...]
+        gram_ref[0:LANES, col_other] = mrx[...]
 
     @pl.when(g < a)
     def _():
-        gram_ref[:, col_owned] = fin[...].T
+        gram_ref[0:LANES, col_owned] = fin[...].T
         mirror.wait_recv()
-        gram_ref[:, col_other] = mrx[...].T
+        gram_ref[0:LANES, col_other] = mrx[...].T
 
     @pl.when(diagonal)
     def _():
-        gram_ref[:, col_owned] = fin[...]
+        gram_ref[0:LANES, col_owned] = fin[...]
         erx[mine] = ext[...]
         for k in range(1, 2 * n_grid):
             q = lax.rem(mine + k, 2 * n_grid)
@@ -354,11 +360,11 @@
 
         @pl.when(x == 0)
         def _():
-            gram_ref[:, col_other] = pair
+            gram_ref[0:LANES, col_other] = pair
 
         @pl.when(x == 1)
         def _():
-            gram_ref[:, col_other] = pair.T
+            gram_ref[0:LANES, col_other] = pair.T
 
     for copy in small + spread:
         copy.wait_send()
@@ -380,6 +386,18 @@
         @pl.when(jnp.logical_or(jnp.logical_not(diagonal), x != k))
         def _():
             extra(k).wait_send()
+
+
+def finish(sums_ref, out_ref, rhs_ref, chi_ref):
+    n_grid = lax.axis_size("grid")
+    out_ref[...] = sums_ref[0:LANES, :]
+    part = rhs_ref.shape[1]
+    rows = sums_ref[LANES : LANES + 8, 0:LANES]
+    index = lax.broadcasted_iota(jnp.int32, (8, LANES), 0)
+    row = jnp.sum(jnp.where(index == lax.axis_index("rows"), rows, 0.0), axis=0, keepdims=True)
+    turn = lax.rem(n_grid - lax.axis_index("grid"), n_grid) * part
+    rhs_ref[...] = pltpu.roll(jnp.broadcast_to(row, (8, LANES)), turn, 1)[0:1, 0:part]
+    chi_ref[...] = sums_ref[sums_ref.shape[0] - 8 : sums_ref.shape[0] - 7, 0:1]
 
 
 def fused(design, observed, weight_class, calib_unit, class_weight, calib_scale):
@@ -394,17 +412,14 @@
     lines = row_count // LANES
     vmem = pl.BlockSpec(memory_space=pltpu.VMEM)
     dma = pltpu.SemaphoreType.DMA
-    gram, aux = pl.pallas_call(
+    sums = pl.pallas_call(
         functools.partial(kernel, (n_rows, n_grid, row_count * n_rows * n_grid)),
-        out_shape=(
-            jax.ShapeDtypeStruct((LANES, 2 * LANES), F32),
-            jax.ShapeDtypeStruct((n_rows + 8, LANES), F32),
-        ),
+        out_shape=jax.ShapeDtypeStruct((LANES + n_rows + 8, 2 * LANES), F32),
         in_specs=[
-            pl.BlockSpec(memory_space=pl.ANY), vmem, vmem, vmem,
+            pl.BlockSpec(memory_space=pltpu.HBM), vmem, vmem, vmem,
             pl.BlockSpec(memory_space=pltpu.SMEM), vmem,
         ],
-        out_specs=(vmem, vmem),
+        out_specs=vmem,
         scratch_shapes=[
             pltpu.VMEM((row_count, width), BF16),
             pltpu.VMEM((row_count, width), BF16),
@@ -444,14 +459,21 @@
         weight_class.reshape(lines, LANES),
         calib_unit.reshape(lines, LANES),
         class_weight,
-        calib_scale,
+        calib_scale.T,
     )
     part = width // (n_rows * n_grid)
-    flat = (lax.axis_index("rows") * n_grid + lax.axis_index("grid")) * part
-    right_hand = lax.dynamic_slice(
-        aux, (flat // LANES, lax.rem(flat, LANES)), (1, part)
-    ).reshape(part)
-    return gram, right_hand, aux[n_rows, 0]
+    gram, right_hand, chi = pl.pallas_call(
+        finish,
+        out_shape=(
+            jax.ShapeDtypeStruct((LANES, 2 * LANES), F32),
+            jax.ShapeDtypeStruct((1, part), F32),
+            jax.ShapeDtypeStruct((1, 1), F32),
+        ),
+        in_specs=[vmem],
+        out_specs=(vmem, vmem, vmem),
+        compiler_params=pltpu.CompilerParams(vmem_limit_bytes=4 * 1024 * 1024),
+    )(sums)
+    return gram, right_hand.reshape(part), chi.reshape(())
 
 
 def local(design, observed, weight_class, calib_unit, class_weight, calib_scale):
@@ -462,6 +484,7 @@
     classes = class_weight.shape[0]
     fits = (
         n_grid == 4
+        and width % (n_rows * n_grid) == 0
         and n_rows == 8
         and width == n_rows * LANES
         and width == blocks * LANES

time: 47.7 us -> 39.5 us (0.83)
  local copies, waits for them, and re-layouts: 5.41 us -> 0.9 us
  Pallas kernels: 41.3 us -> 37.7 us
    pallas_call x1, Pallas kernels: 41.3 us -> 37.1 us  [fused(): pl.pallas_call(functools.partial(kernel, (n_rows, n_grid, row_count * n_r...]
    unnamed x2, local copies, waits for them, and re-layouts: 2.95 us -> 0.9 us
    reshape x1 -> x0, local copies, waits for them, and re-layouts: 1.27 us -> none  [fused(): right_hand = lax.dynamic_slice(aux, (flat // LANES, lax.rem(flat, LANES))...]
    slice x1 -> x0, local copies, waits for them, and re-layouts: 1.19 us -> none  [fused(): return (gram, right_hand, aux[n_rows, 0])]
    pallas_call x0 -> x1, Pallas kernels: none -> 0.67 us  [fused(): pl.pallas_call(finish, out_shape=(jax.ShapeDtypeStruct((LANES, 2 * LANES)...]
where the time goes in v2:
time: 39.5 us; the launch traced here: 39.3 us
  Pallas kernels  37.7 us (95%)
  local copies, waits for them, and re-layouts  0.9 us (2%)
  between operations  0.65 us (2%)
    pallas_call x1, Pallas kernels, fused(): pl.pallas_call(functools.partial(kernel, (n_rows, n_grid, row_count * n_r...  37.1 us
    unnamed x2, local copies, waits for them, and re-layouts  0.9 us

profile of v2, /device:TPU:4, one launch (start us, length us, event | category | flops | bytes accessed | tf_op | source)
XLA Modules:
  0.0 39.3 jit_solution(4733946445929807154)
XLA Ops:
  0.6 37.1 %shard_map.85.sums_ref = f32[144,256]{1,0:T(8,128)} custom-call(bf16[3072,1024]{1,0:T(8,128)(2,1)} %design_hbm.1, f32[24,128]{1,0:T(8,128)} %bitcast.6, s32[24,128]{1,0:T(8,128)} %bitcast.7, s32[24,128]{1,0:T(8,128)} %bitcast.8, f32[16]{0:T(128)} %cw_ref.1, f32[8,64]{1,0:T(8,128)} %bitcast.9), custom_call_target="tpu_custom_call" | custom-call | tf_op jit(solution)/shard_map/pallas_call | solution.py:415
  37.7 0.0 copy-start
  37.7 0.9 %copy-done = f32[144,256]{1,0:T(8,128)S(1)} copy-done((f32[144,256]{1,0:T(8,128)S(1)}, f32[144,256]{1,0:T(8,128)}, u32[]{:S(2)}) %copy-start) | copy-done | bytes 147480
  38.6 0.7 %shard_map.86 = (f32[128,256]{1,0:T(8,128)}, f32[1,32]{1,0:T(1,128)}, f32[1,1]{1,0:T(1,128)}) custom-call(f32[144,256]{1,0:T(8,128)S(1)} %copy-done), custom_call_target="tpu_custom_call" | custom-call | tf_op jit(solution)/shard_map/pallas_call | solution.py:465
Async XLA Ops:
  37.7 0.9 %copy-start = (f32[144,256]{1,0:T(8,128)S(1)}, f32[144,256]{1,0:T(8,128)}, u32[]{:S(2)}) copy-start(f32[144,256]{1,0:T(8,128)} %shard_map.85.sums_ref) | copy-start | bytes 442372

commit v3 on v2

--- a/solution.py
+++ b/solution.py
@@ -283,6 +283,7 @@
     stage2(0)
     stage1(2)
     stage2(1)
+    stage2(3)
     stage3(0)
     small_step(3, None)
     spread = []
@@ -292,9 +293,8 @@
         )
         copy.start()
         spread.append(copy)
-    stage2(3)
+    stage2(2)
     stage3(1)
-    stage2(2)
     stage3(3)
     stage3(2)
 

time: 39.5 us -> 39 us (0.987)
  Pallas kernels: 37.7 us -> 37.2 us
    pallas_call x1, Pallas kernels: 37.1 us -> 36.5 us  [fused(): pl.pallas_call(functools.partial(kernel, (n_rows, n_grid, row_count * n_r...]
where the time goes in v3:
time: 39 us; the launch traced here: 38.7 us
  Pallas kernels  37.2 us (95%)
  local copies, waits for them, and re-layouts  0.9 us (2%)
  between operations  0.65 us (2%)
    pallas_call x1, Pallas kernels, fused(): pl.pallas_call(functools.partial(kernel, (n_rows, n_grid, row_count * n_r...  36.5 us
    unnamed x2, local copies, waits for them, and re-layouts  0.9 us

profile of v3, /device:TPU:4, one launch (start us, length us, event | category | flops | bytes accessed | tf_op | source)
XLA Modules:
  0.0 38.7 jit_solution(9166440143290124934)
XLA Ops:
  0.6 36.5 %shard_map.85.sums_ref = f32[144,256]{1,0:T(8,128)} custom-call(bf16[3072,1024]{1,0:T(8,128)(2,1)} %design_hbm.1, f32[24,128]{1,0:T(8,128)} %bitcast.6, s32[24,128]{1,0:T(8,128)} %bitcast.7, s32[24,128]{1,0:T(8,128)} %bitcast.8, f32[16]{0:T(128)} %cw_ref.1, f32[8,64]{1,0:T(8,128)} %bitcast.9), custom_call_target="tpu_custom_call" | custom-call | tf_op jit(solution)/shard_map/pallas_call | solution.py:415
  37.2 0.0 copy-start
  37.2 0.9 %copy-done = f32[144,256]{1,0:T(8,128)S(1)} copy-done((f32[144,256]{1,0:T(8,128)S(1)}, f32[144,256]{1,0:T(8,128)}, u32[]{:S(2)}) %copy-start) | copy-done | bytes 147480
  38.1 0.7 %shard_map.86 = (f32[128,256]{1,0:T(8,128)}, f32[1,32]{1,0:T(1,128)}, f32[1,1]{1,0:T(1,128)}) custom-call(f32[144,256]{1,0:T(8,128)S(1)} %copy-done), custom_call_target="tpu_custom_call" | custom-call | tf_op jit(solution)/shard_map/pallas_call | solution.py:465
Async XLA Ops:
  37.2 0.9 %copy-start = (f32[144,256]{1,0:T(8,128)S(1)}, f32[144,256]{1,0:T(8,128)}, u32[]{:S(2)}) copy-start(f32[144,256]{1,0:T(8,128)} %shard_map.85.sums_ref) | copy-start | bytes 442372
